TPU v7x, 16 devices: a 4x2x1 block of a 4x4x4 slice. The times are simulated.
16 devices in a mesh: dp: 4 (over y, z, core), tp: 4 (over x).
Axes of the slice: x: 4, y: 2, z: 1, core: 2. Of those that a mesh axis runs over, the one named last changes fastest.
The devices are a block of a 4x4x4 slice.
Arguments:
- x: bfloat16 [2560, 6656], P(('dp', 'tp')), parts along dimension 0
- dy: bfloat16 [2560, 6656], P(('dp', 'tp')), parts along dimension 0
- gate: bfloat16 [2560, 17920], P('dp', 'tp'), parts along dimension 0
- up: bfloat16 [2560, 17920], P('dp', 'tp'), parts along dimension 0
- w_gate: bfloat16 [6656, 17920], P(None, 'tp')
- w_up: bfloat16 [6656, 17920], P(None, 'tp')
- w_down: bfloat16 [17920, 6656], P('tp')
Outputs:
- output 1: bfloat16 [2560, 6656], P(('dp', 'tp')), parts along dimension 0
- output 2: bfloat16 [26624, 17920], P('dp', 'tp'), parts along dimension 0
- output 3: bfloat16 [26624, 17920], P('dp', 'tp'), parts along dimension 0
- output 4: bfloat16 [71680, 6656], P(('dp', 'tp')), parts along dimension 0
There are 4 independent parts. A program takes and returns all parts, laid end to end along the dimension named above; an argument that names none is the same for every part.
All inputs are finite; a program needn't handle non-finite values.
Results may differ from a plain program's by a relative error of at most 0.012.
Values are sent between devices in bfloat16 or wider.
A program may use at most 1.5 GiB of HBM per device.

v0:
```python
import jax
import jax.numpy as jnp


def act(gate, up):
    return jax.nn.silu(gate) * up


def solution(mesh):
    def step(x, dy, gate, up, w_gate, w_up, w_down):
        hidden, back = jax.vjp(act, gate.astype(jnp.float32), up.astype(jnp.float32))
        d_hidden = jnp.dot(dy, w_down.T, preferred_element_type=jnp.float32)
        d_gate, d_up = (g.astype(jnp.bfloat16) for g in back(d_hidden))
        dx = jnp.dot(d_gate, w_gate.T) + jnp.dot(d_up, w_up.T)
        groups = mesh.shape["dp"]

        def by_group(a, b):
            a, b = (t.reshape(groups, -1, t.shape[-1]) for t in (a, b))
            product = jnp.einsum("gta,gtb->gab", a, b, preferred_element_type=jnp.float32)
            return product.astype(jnp.bfloat16).reshape(-1, b.shape[-1])

        return dx, by_group(x, d_gate), by_group(x, d_up), by_group(hidden.astype(jnp.bfloat16), dy)

    return step
```

profile of v0, /device:TPU:112, one launch (start us, length us, event | category | flops | bytes accessed | tf_op | source)
XLA Modules:
  0.0 723.6 jit_solution(17770615355311153658)
XLA Ops:
  7.2 0.1 all-gather.9.cloned.1.call-start
  7.2 0.7 all-gather.9.cloned.1.call-update
  8.0 0.1 all-gather.11.cloned.1.call-start
  8.0 2.4 collective-permute-start
  10.5 1.6 collective-permute-start.1
  12.1 0.1 all-gather.11.cloned.1.call-update
  12.2 0.1 reduce-scatter.4.cloned.1.call-start
  12.2 1.2 dynamic-slice.27
  16.1 77.3 %collective-permute-done = bf16[1,1,160,6656]{3,2,1,0:T(8,128)(2,1)} collective-permute-done((bf16[1,1,160,6656]{3,2,1,0:T(8,128)(2,1)}, bf16[1,1,160,6656]{3,2,1,0:T(8,128)(2,1)}, u32[]{:S(2)}, u32[]{:S(2)}) %collective-permute-start) | collective-permute-done | bytes 2129952 | tf_op jit(solution)/gta,gtb->gab/dot_general | solution.py:19
  93.4 1.7 collective-permute-start.2
  95.1 63.0 %all-gather.9.cloned.1.call-done = bf16[640,6656]{1,0:T(8,128)(2,1)} async-done(((bf16[160,6656]{1,0:T(8,128)(2,1)}), bf16[640,6656]{1,0:T(8,128)(2,1)}) %all-gather.9.cloned.1.call-update) | async-done | bytes 8519696 | tf_op args[1]
  158.1 48.3 %fusion.26 = f32[640,4480]{1,0:T(8,128)} fusion(bf16[640,6656]{1,0:T(8,128)(2,1)} %all-gather.9.cloned.1.call-done, bf16[4480,6656]{1,0:T(8,128)(2,1)} %param.3), kind=kOutput, calls=%fused_computation.41 | convolution fusion | flops 38168166400 | bytes 79626240 | tf_op jit(solution)/dot_general | solution.py:12
  206.4 13.3 %fusion.10 = (bf16[1,1,640,4480]{3,2,1,0:T(8,128)(2,1)}, bf16[640,4480]{1,0:T(8,128)(2,1)S(1)}) fusion(bf16[640,4480]{1,0:T(8,128)(2,1)} %param.4, bf16[640,4480]{1,0:T(8,128)(2,1)} %param.5, f32[640,4480]{1,0:T(8,128)} %fusion.26), kind=kLoop, calls=%fused_computation.25 | loop fusion | flops 45875200 | bytes 34406400 | tf_op jit(solution)/gta,gtb->gab/dot_general | solution.py:19
  219.7 2.5 copy-done
  222.2 46.8 %fusion.27 = bf16[640,6656]{1,0:T(8,128)(2,1)} fusion(bf16[640,4480]{1,0:T(8,128)(2,1)S(1)} %get-tuple-element.17, bf16[6656,4480]{1,0:T(8,128)(2,1)} %param.6), kind=kOutput, calls=%fused_computation.42 | convolution fusion | flops 38168166400 | bytes 73891840 | tf_op jit(solution)/dot_general | solution.py:14
  269.0 67.5 %convolution_add_fusion = bf16[640,6656]{1,0:T(8,128)(2,1)} fusion(bf16[640,6656]{1,0:T(8,128)(2,1)} %fusion.27, bf16[6656,4480]{1,0:T(8,128)(2,1)} %param.7, f32[640,4480]{1,0:T(8,128)} %fusion.26, bf16[640,4480]{1,0:T(8,128)(2,1)} %param.5), kind=kOutput, calls=%fused_computation.24 | convolution fusion | flops 38192496640 | bytes 93880320 | tf_op jit(solution)/dot_general | solution.py:14
  336.6 0.1 reduce-scatter.4.cloned.1.call-update
  336.6 0.0 all-gather.11.cloned.1.call-done
  336.6 56.6 %fusion.2 = bf16[6656,4480]{0,1:T(8,128)(2,1)} fusion(bf16[640,6656]{1,0:T(8,128)(2,1)} %all-gather.11.cloned.1.call-done, f32[640,4480]{1,0:T(8,128)} %fusion.26, bf16[640,4480]{1,0:T(8,128)(2,1)} %param.5), kind=kOutput, calls=%fused_computation.5 | convolution fusion | flops 38218055680 | bytes 85360640 | tf_op jit(solution)/gta,gtb->gab/dot_general | solution.py:19
  393.2 56.3 %fusion.1 = bf16[6656,4480]{0,1:T(8,128)(2,1)} fusion(bf16[640,4480]{1,0:T(8,128)(2,1)} %copy-done, bf16[640,6656]{1,0:T(8,128)(2,1)} %all-gather.11.cloned.1.call-done), kind=kOutput, calls=%fused_computation.4 | convolution fusion | flops 38197985280 | bytes 73891840 | tf_op jit(solution)/gta,gtb->gab/dot_general | solution.py:19
  449.5 45.6 %fusion.11 = f32[4480,6656,1]{1,0,2:T(8,128)} fusion(bf16[1,1,160,6656]{3,2,1,0:T(8,128)(2,1)} %collective-permute-done, bf16[1,1,160,6656]{3,2,1,0:T(8,128)(2,1)S(1)} %bitcast.67, s32[]{:T(128)} %bitcast.8, bf16[1,1,640,4480]{3,2,1,0:T(8,128)(2,1)} %get-tuple-element.16, s32[]{:T(128)} %bitcast.9), kind=kOutput, calls=%fused_computation.27 | convolution fusion | flops 19091947520 | bytes 129269768 | tf_op jit(solution)/gta,gtb->gab/dot_general | solution.py:19
  495.1 77.8 %copy = bf16[6656,4480]{1,0:T(8,128)(2,1)} copy(bf16[6656,4480]{0,1:T(8,128)(2,1)} %fusion.1) | data formatting | bytes 119275520
  572.9 77.8 %copy.1 = bf16[6656,4480]{1,0:T(8,128)(2,1)} copy(bf16[6656,4480]{0,1:T(8,128)(2,1)} %fusion.2) | data formatting | bytes 119275520
  650.7 66.1 %fusion = bf16[4480,6656]{1,0:T(8,128)(2,1)} fusion(f32[4480,6656,1]{1,0,2:T(8,128)} %fusion.11, bf16[1,1,160,6656]{3,2,1,0:T(8,128)(2,1)} %collective-permute-done.2, bf16[1,1,160,6656]{3,2,1,0:T(8,128)(2,1)} %collective-permute-done.1, s32[]{:T(128)} %bitcast.14, bf16[1,1,640,4480]{3,2,1,0:T(8,128)(2,1)} %get-tuple-element.16, s32[]{:T(128)} %bitcast.15), kind=kOutput, calls=%fused_computation.1 | convolution fusion | flops 19151585280 | bytes 188907520 | tf_op jit(solution)/gta,gtb->gab/dot_general | solution.py:19
  (6 shorter events, 0.0 us)
Async XLA Ops:
  7.2 151.0 %all-gather.9.cloned.1.call-start = ((), (), s32[]{:S(2)}) async-start(), calls=%async_computation.1 | async-start | bytes 10649600 | tf_op args[1]
  8.0 328.7 %all-gather.11.cloned.1.call-start = ((), (), s32[]{:S(2)}) async-start(), calls=%async_computation.2 | async-start | bytes 10649600 | tf_op jit(solution)/reshape | solution.py:18
  8.0 85.3 %collective-permute-start = (bf16[1,1,160,6656]{3,2,1,0:T(8,128)(2,1)}, bf16[1,1,160,6656]{3,2,1,0:T(8,128)(2,1)}, u32[]{:S(2)}, u32[]{:S(2)}) collective-permute-start(bf16[1,1,160,6656]{3,2,1,0:T(8,128)(2,1)} %bitcast.65), channel_id=9, source_target_pairs={{0,1},{1,2},{2,3},{3,0},{4,5},{5,6},{6,7},{7,4},{8,9},{9,10},{10,1... | collective-permute-start | bytes 6389768 | tf_op jit(solution)/gta,gtb->gab/dot_general | solution.py:19
  10.5 640.2 %collective-permute-start.1 = (bf16[1,1,160,6656]{3,2,1,0:T(8,128)(2,1)}, bf16[1,1,160,6656]{3,2,1,0:T(8,128)(2,1)}, u32[]{:S(2)}, u32[]{:S(2)}) collective-permute-start(bf16[1,1,160,6656]{3,2,1,0:T(8,128)(2,1)} %bitcast.66), channel_id=10, source_target_pairs={{0,3},{1,0},{2,1},{3,2},{4,7},{5,4},{6,5},{7,6},{8,11},{9,8},{10,9... | collective-permute-start | bytes 6389768 | tf_op jit(solution)/gta,gtb->gab/dot_general | solution.py:19
  12.2 704.6 %reduce-scatter.4.cloned.1.call-start = ((), (), s32[]{:S(2)}) async-start(), calls=%async_computation.3 | async-start | bytes 10649600
  93.4 557.3 %collective-permute-start.2 = (bf16[1,1,160,6656]{3,2,1,0:T(8,128)(2,1)}, bf16[1,1,160,6656]{3,2,1,0:T(8,128)(2,1)}, u32[]{:S(2)}, u32[]{:S(2)}) collective-permute-start(bf16[1,1,160,6656]{3,2,1,0:T(8,128)(2,1)} %collective-permute-done), channel_id=11, source_target_pairs={{0,1},{1,2},{2,3},{3,0},{4,5},{5,6},{6,7},{7,4},{8,9},{9,10},{10,1... | collective-permute-start | bytes 6389768 | tf_op jit(solution)/gta,gtb->gab/dot_general | solution.py:19
  219.7 2.5 copy-start
  393.2 56.3 %copy-start.1 = (bf16[160,6656]{1,0:T(8,128)(2,1)S(1)}, bf16[160,6656]{1,0:T(8,128)(2,1)}, u32[]{:S(2)}) copy-start(bf16[160,6656]{1,0:T(8,128)(2,1)} %param.2) | copy-start | bytes 6389764
Sparse Core Ops, SparseCore 0:
  9.6 148.5 all-gather.8
  159.7 81.5 all-gather.10
  336.7 77.9 reduce-scatter.3
where the time goes:
time: 734 us; the launch traced here: 724 us
  matrix products  387 us (53%)
  local copies, waits for them, and re-layouts  159 us (22%)
  waiting for transfers between devices  141 us (19%)
  between operations  16.6 us (2%)
  other arithmetic  13.3 us (2%)
    dot_general x4, matrix products, by_group(): jnp.einsum('gta,gtb->gab', a, b, preferred_element_type=jnp.float32)  225 us
    unnamed x6, local copies, waits for them, and re-layouts  158 us
    dot_general x2, matrix products, step(): dx = jnp.dot(d_gate, w_gate.T) + jnp.dot(d_up, w_up.T)  114 us
    dot_general x3, waiting for transfers between devices, by_group(): jnp.einsum('gta,gtb->gab', a, b, preferred_element_type=jnp.float32)  77.3 us
    unnamed x5, waiting for transfers between devices  63.9 us
    dot_general x1, matrix products, step(): d_hidden = jnp.dot(dy, w_down.T, preferred_element_type=jnp.float32)  48.3 us
  transfers between devices with their start and end apart: 6, of which 2 were waited for; matrix products, arithmetic and copies ran while one was open for 77% of the time, Pallas kernels for 0%

commit v1 on v0

v1 whole, which is shorter than its diff:
```python
import functools

import jax
import jax.numpy as jnp
from jax import lax
from jax.experimental import pallas as pl
from jax.experimental.pallas import tpu as pltpu
from jax.sharding import PartitionSpec as P

MESH = pl.DeviceIdType.MESH
BF16, F32 = jnp.bfloat16, jnp.float32
BLK = 512
LATE = 3
ROWS = 16
VMEM_LIMIT = 66_500_000

NT = (((1,), (1,)), ((), ()))
NN = (((1,), (0,)), ((), ()))


def dot(a, b, dims):
    return lax.dot_general(a, b, dims, preferred_element_type=F32)


def act_parts(gate, up):
    g, u = gate.astype(F32), up.astype(F32)
    s = 1.0 / (1.0 + jnp.exp(-g))
    return g, u, s


def fused_kernel(
    n, x_own, dy_own, gate, up, wg, wu, wd,
    dwd, dcat_out, dxp, xg,
    dyg, dcat, acc, hid, wb, gu,
    d_send, d_recv, d_own, x_send, x_recv, x_in, x_out, w_sem, w_last, o_sem, l_sem, gu_sem, dx_sem, dc_sem,
):
    own, depth = dy_own.shape
    rows, ff = gate.shape
    nb = depth // BLK
    nf, rem = ff // BLK, ff % BLK
    half = own // 2
    side = BLK - rem
    tail = rem - side
    np1 = nf + 1
    me = lax.axis_index("tp")
    right, left = lax.rem(me + 1, n), lax.rem(me + n - 1, n)

    def cols(b):
        return pl.ds(pl.multiple_of(b * BLK, BLK), BLK)

    def own_rows(i):
        return pl.ds(pl.multiple_of(i * own, 16), own)

    def half_rows(i, second):
        return pl.ds(pl.multiple_of(i * own + second * half, 16), half)

    def remote(src, dst, send, recv, to):
        return pltpu.make_async_remote_copy(
            src_ref=src, dst_ref=dst, send_sem=send, recv_sem=recv, device_id={"tp": to}, device_id_type=MESH
        )

    def view(which, b, r):
        return dyg.at[b, r] if which == "d" else xg.at[r, cols(b)]

    def sems(which):
        return (d_send, d_recv) if which == "d" else (x_send, x_recv)

    def hop_copy(which, b, i):
        src = (dy_own if which == "d" else x_own).at[:, cols(b)]
        send, recv = sems(which)
        return remote(src, view(which, b, own_rows(me)), send.at[b, i], recv.at[b, i], (right, left)[i])

    def fwd_copy(which, b, i):
        r = half_rows((left, right)[i], i)
        send, recv = sems(which)
        return remote(view(which, b, r), view(which, b, r), send.at[b, 2 + i], recv.at[b, 2 + i], (right, left)[i])

    def hop(which, b):
        for i in (0, 1):
            hop_copy(which, b, i).start()

    def fwd(which, b):
        for i in (0, 1):
            r = own_rows((left, right)[i])
            send, recv = sems(which)
            remote(view(which, b, r), view(which, b, r), send.at[b, i], recv.at[b, i], right).wait_recv()
            fwd_copy(which, b, i).start()

    def far(which, b):
        opposite = lax.rem(me + 2, n)
        send, recv = sems(which)
        for i in (0, 1):
            r = half_rows(opposite, i)
            remote(view(which, b, r), view(which, b, r), send.at[b, 2 + i], recv.at[b, 2 + i], right).wait_recv()

    def sent(which, b):
        for i in (0, 1):
            hop_copy(which, b, i).wait_send()
            fwd_copy(which, b, i).wait_send()

    def own_copy(b):
        return pltpu.make_async_copy(dy_own.at[:, cols(b)], dyg.at[b, own_rows(me)], d_own.at[b])

    def size(p):
        return BLK if p < nf else rem

    def wd_copies(b, s):
        return [
            pltpu.make_async_copy(
                wd.at[pl.ds(p * BLK, size(p)), cols(b)], wb.at[s, p, pl.ds(0, size(p))], w_sem.at[s, p]
            )
            for p in range(np1)
        ]

    def out_copies(b, s):
        return [
            pltpu.make_async_copy(
                wb.at[s, np1 + p, pl.ds(0, size(p))], dwd.at[pl.ds(p * BLK, size(p)), cols(b)], o_sem.at[s, p]
            )
            for p in range(np1)
        ]

    def wx_copies(b, s):
        r = cols(b)
        c = [
            pltpu.make_async_copy((wg, wu)[i].at[r, pl.ds(p * BLK, BLK)], wb.at[s, i * nf + p], w_sem.at[s, i * nf + p])
            for i in (0, 1)
            for p in range(nf)
        ]
        e = nf * BLK
        c.append(
            pltpu.make_async_copy(wg.at[r, pl.ds(e, rem)], wb.at[s, 2 * nf, :, pl.ds(0, rem)], w_sem.at[s, 2 * nf])
        )
        c.append(
            pltpu.make_async_copy(wu.at[r, pl.ds(e, side)], wb.at[s, 2 * nf, :, pl.ds(rem, side)], w_last.at[s])
        )
        c.append(
            pltpu.make_async_copy(
                wu.at[r, pl.ds(e + side, tail)], wb.at[s, 2 * nf + 1, :, pl.ds(0, tail)], w_sem.at[s, 2 * nf + 1]
            )
        )
        return c

    def gu_copies(p, s, width):
        c = pl.ds(pl.multiple_of(p * BLK, BLK), width)
        return [
            pltpu.make_async_copy((gate, up)[i].at[:, c], gu.at[2 * s + i, :, pl.ds(0, width)], gu_sem.at[s, i])
            for i in (0, 1)
        ]

    def late_copies(p, q, width):
        r = pl.ds(pl.multiple_of(p * BLK, BLK), width)
        return [
            pltpu.make_async_copy(
                wb.at[1, np1 + LATE * q + k, pl.ds(0, width)], dwd.at[r, cols(nb - LATE + k)], l_sem.at[q, k]
            )
            for k in range(LATE)
        ]

    def start(copies):
        for c in copies:
            c.start()

    def wait(copies):
        for c in copies:
            c.wait()

    barrier = pltpu.get_barrier_semaphore()
    for to in (left, right):
        pl.semaphore_signal(barrier, inc=1, device_id={"tp": to}, device_id_type=MESH)
    start(gu_copies(0, 0, BLK))
    start(gu_copies(1, 1, BLK))
    pl.semaphore_wait(barrier, 2)
    for b in range(3):
        hop("d", b)
    for b in range(nb):
        own_copy(b).start()
    start(wd_copies(0, 0))
    start(wd_copies(1, 1))

    def hidden_piece(p, s, width):
        wait(gu_copies(p, s, width))
        for r in range(0, rows, 128):
            for c in range(0, width, 128):
                g, u, sg = act_parts(gu[2 * s, r : r + 128, c : c + 128], gu[2 * s + 1, r : r + 128, c : c + 128])
                hid[p, c : c + 128, r : r + 128] = (g * sg * u).astype(BF16).T
        acc[p, :, :width] = jnp.zeros((rows, width), F32)

    def hidden_full(p, _):
        s = lax.rem(p, 2)
        hidden_piece(p, s, BLK)

        @pl.when(p < nf - 2)
        def _():
            start(gu_copies(p + 2, s, BLK))

        @pl.when(p == nf - 2)
        def _():
            start(gu_copies(nf, s, rem))

        return 0

    lax.fori_loop(0, nf // 2, hidden_full, 0)
    fwd("d", 0)
    hop("d", 3)
    lax.fori_loop(nf // 2, nf, hidden_full, 0)
    hidden_piece(nf, nf % 2, rem)
    fwd("d", 1)
    hop("d", 4)

    def d_hidden(b, s):
        dyb = dyg[b]
        for p in range(np1):
            w = size(p)
            acc[p, :, :w] += dot(dyb, wb[s, p, :w, :], NT)

    def both(b, _):
        s = lax.rem(b, 2)
        fwd("d", b + 2)

        @pl.when(b < nb - 5)
        def _():
            hop("d", b + 5)

        wait(wd_copies(b, s))
        own_copy(b).wait()
        far("d", b)

        @pl.when(b >= 2)
        def _():
            wait(out_copies(b - 2, s))

        d_hidden(b, s)
        dyb = dyg[b]
        for p in range(np1):
            w = size(p)
            wb[s, np1 + p, :w, :] = dot(hid[p, :w, :], dyb, NN).astype(BF16)
        start(out_copies(b, s))
        start(wd_copies(b + 2, s))
        return 0

    lax.fori_loop(0, nb - LATE, both, 0)

    start(gu_copies(0, 0, BLK))
    start(gu_copies(1, 1, BLK))

    def only_hidden(b, _):
        s = lax.rem(b, 2)

        @pl.when(b == nb - 3)
        def _():
            fwd("d", nb - 1)

        wait(wd_copies(b, s))
        own_copy(b).wait()
        far("d", b)
        d_hidden(b, s)

        @pl.when(b == nb - 3)
        def _():
            start(wd_copies(nb - 1, s))

        return 0

    lax.fori_loop(nb - LATE, nb, only_hidden, 0)
    for b in (nb - LATE - 2, nb - LATE - 1):
        wait(out_copies(b, b % 2))
    start(wx_copies(0, 0))
    for b in range(3):
        hop("x", b)

    def act_piece(p, s, width, first):
        wait(gu_copies(p, s, width))
        if first is None:
            wait(late_copies(p - 2, s, BLK))
        else:

            @pl.when(first)
            def _():
                wait(late_copies(p - 2, s, BLK))

        for r in range(0, rows, ROWS):
            t = slice(r, r + ROWS)
            g, u, sg = act_parts(gu[2 * s, t, :width], gu[2 * s + 1, t, :width])
            dh = acc[p, t, :width]
            silu = g * sg
            d_up = (dh * silu).astype(BF16)
            d_gate = (dh * u * (sg + silu * (1.0 - sg))).astype(BF16)
            if width == BLK:
                dcat[p, t, :] = d_gate
                dcat[nf + p, t, :] = d_up
            else:
                dcat[2 * nf, t, :rem] = d_gate
                dcat[2 * nf, t, rem:] = d_up[:, :side]
                dcat[2 * nf + 1, t, :tail] = d_up[:, side:]
        for k in range(LATE):
            wb[1, np1 + LATE * s + k, :width, :] = dot(hid[p, :width, :], dyg[nb - LATE + k], NN).astype(BF16)
        start(late_copies(p, s, width))

    def act_full(p, _):
        s = lax.rem(p, 2)
        act_piece(p, s, BLK, p >= 2)

        @pl.when(p < nf - 2)
        def _():
            start(gu_copies(p + 2, s, BLK))

        @pl.when(p == nf - 2)
        def _():
            start(gu_copies(nf, s, rem))

        return 0

    lax.fori_loop(0, nf, act_full, 0)
    act_piece(nf, nf % 2, rem, None)
    wait(late_copies(nf - 1, (nf - 1) % 2, BLK))
    wait(late_copies(nf, nf % 2, rem))
    start(wx_copies(1, 1))

    def dcat_copies():
        c = [pltpu.make_async_copy(dcat.at[p], dcat_out.at[p], dc_sem.at[p]) for p in range(2 * nf + 1)]
        c.append(
            pltpu.make_async_copy(
                dcat.at[2 * nf + 1, :, pl.ds(0, tail)], dcat_out.at[2 * nf + 1, :, pl.ds(0, tail)], dc_sem.at[2 * nf + 1]
            )
        )
        return c

    start(dcat_copies())

    def dx_copy(b, s):
        return pltpu.make_async_copy(gu.at[s], dxp.at[:, cols(b)], dx_sem.at[s])

    def x_in_copy(b, s):
        return pltpu.make_async_copy(x_own.at[:, cols(b)], gu.at[2 + s, pl.ds(0, own)], x_in.at[s])

    def x_out_copy(b, s):
        return pltpu.make_async_copy(gu.at[2 + s, pl.ds(0, own)], xg.at[own_rows(me), cols(b)], x_out.at[s])

    x_in_copy(0, 0).start()

    def dx_block(b, _):
        s = lax.rem(b, 2)
        fwd("x", b)

        @pl.when(b < nb - 3)
        def _():
            hop("x", b + 3)

        x_in_copy(b, s).wait()
        x_out_copy(b, s).start()

        @pl.when(b >= 1)
        def _():
            x_out_copy(b - 1, 1 - s).wait()

        @pl.when(b < nb - 1)
        def _():
            x_in_copy(b + 1, 1 - s).start()

        @pl.when(b >= 2)
        def _():
            dx_copy(b - 2, s).wait()

        wait(wx_copies(b, s))
        total = dot(dcat[0], wb[s, 0], NT)
        for p in range(1, 2 * nf + 1):
            total += dot(dcat[p], wb[s, p], NT)
        total += dot(dcat[2 * nf + 1, :, :tail], wb[s, 2 * nf + 1, :, :tail], NT)
        gu[s] = total.astype(BF16)
        dx_copy(b, s).start()

        @pl.when(b < nb - 2)
        def _():
            start(wx_copies(b + 2, s))

        return 0

    lax.fori_loop(0, nb, dx_block, 0)

    for b in (nb - 2, nb - 1):
        dx_copy(b, b % 2).wait()
    x_out_copy(nb - 1, (nb - 1) % 2).wait()
    wait(dcat_copies())

    def drain(b, _):
        far("x", b)
        sent("x", b)
        sent("d", b)
        return 0

    lax.fori_loop(0, nb, drain, 0)


def fused(n, x, dy, gate, up, wg, wu, wd):
    own, depth = x.shape
    rows, ff = gate.shape
    nb, nf, rem = depth // BLK, ff // BLK, ff % BLK
    np1, np2 = nf + 1, 2 * nf + 2
    dma = pltpu.SemaphoreType.DMA
    hbm = pl.BlockSpec(memory_space=pl.ANY)
    flops = 2 * rows * depth * ff * 4
    return pl.pallas_call(
        functools.partial(fused_kernel, n),
        out_shape=[
            jax.ShapeDtypeStruct((ff, depth), BF16),
            jax.ShapeDtypeStruct((np2, rows, BLK), BF16),
            jax.ShapeDtypeStruct((rows, depth), BF16),
            jax.ShapeDtypeStruct((rows, depth), BF16),
        ],
        in_specs=[hbm] * 7,
        out_specs=[hbm] * 4,
        scratch_shapes=[
            pltpu.VMEM((nb, rows, BLK), BF16),
            pltpu.VMEM((np2, rows, BLK), BF16),
            pltpu.VMEM((np1, rows, BLK), F32),
            pltpu.VMEM((np1, BLK, rows), BF16),
            pltpu.VMEM((2, np2, BLK, BLK), BF16),
            pltpu.VMEM((4, rows, BLK), BF16),
            dma((nb, 4)), dma((nb, 4)), dma((nb,)), dma((nb, 4)), dma((nb, 4)), dma((2,)), dma((2,)),
            dma((2, np2)), dma((2,)), dma((2, np1)), dma((2, LATE)), dma((2, 2)), dma((2,)), dma((np2,)),
        ],
        compiler_params=pltpu.CompilerParams(collective_id=0, has_side_effects=True, vmem_limit_bytes=VMEM_LIMIT),
        cost_estimate=pl.CostEstimate(flops=flops, bytes_accessed=5 * ff * depth * 2, transcendentals=0),
        name="fused",
    )(x, dy, gate, up, wg, wu, wd)


def weights_kernel(x_ref, dcat_ref, dwd_ref, og, ou, od):
    ff = og.shape[1]
    nf, rem = ff // BLK, ff % BLK
    side = BLK - rem
    e = nf * BLK
    xt = x_ref[...].T
    for p in range(nf):
        og[:, p * BLK : (p + 1) * BLK] = dot(xt, dcat_ref[p], NN).astype(BF16)
        ou[:, p * BLK : (p + 1) * BLK] = dot(xt, dcat_ref[nf + p], NN).astype(BF16)
    both = dot(xt, dcat_ref[2 * nf], NN).astype(BF16)
    og[:, e:] = both[:, :rem]
    ou[:, e : e + side] = both[:, rem:]
    ou[:, e + side :] = dot(xt, dcat_ref[2 * nf + 1, :, : rem - side], NN).astype(BF16)
    od[...] = dwd_ref[...]


def weights(xg, dcat, dwd):
    rows, depth = xg.shape
    ff = dwd.shape[0]
    nb = depth // BLK
    return pl.pallas_call(
        weights_kernel,
        grid=(nb,),
        in_specs=[
            pl.BlockSpec((rows, BLK), lambda i: (0, i)),
            pl.BlockSpec(dcat.shape, lambda i: (0, 0, 0), pipeline_mode=pl.Buffered(1)),
            pl.BlockSpec((ff, BLK), lambda i: (0, i)),
        ],
        out_specs=[
            pl.BlockSpec((BLK, ff), lambda i: (i, 0)),
            pl.BlockSpec((BLK, ff), lambda i: (i, 0)),
            pl.BlockSpec((ff, BLK), lambda i: (0, i)),
        ],
        out_shape=[
            jax.ShapeDtypeStruct((depth, ff), BF16),
            jax.ShapeDtypeStruct((depth, ff), BF16),
            jax.ShapeDtypeStruct((ff, depth), BF16),
        ],
        compiler_params=pltpu.CompilerParams(vmem_limit_bytes=VMEM_LIMIT),
        cost_estimate=pl.CostEstimate(flops=2 * rows * depth * ff * 2, bytes_accessed=4 * ff * depth * 2, transcendentals=0),
        name="weights",
    )(xg, dcat, dwd)


def solution(mesh):
    n = mesh.shape["tp"]

    def step(x, dy, gate, up, wg, wu, wd):
        dwd, dcat, dxp, xg = fused(n, x, dy, gate, up, wg, wu, wd)
        dx = lax.psum_scatter(dxp, "tp", scatter_dimension=0, tiled=True)
        dwg, dwu, dwd = weights(xg, dcat, dwd)
        return dx, dwg, dwu, dwd

    tokens, inner, both = P(("dp", "tp"), None), P("dp", "tp"), P(None, "tp")
    return jax.shard_map(
        step,
        mesh=mesh,
        in_specs=(tokens, tokens, inner, inner, both, both, P("tp", None)),
        out_specs=(tokens, inner, inner, tokens),
        check_vma=False,
    )
```

time: 734 us -> 334 us (0.46); the launches traced: 724 us -> 334 us
  matrix products: 387 us -> 0 us
  Pallas kernels: 0 us -> 320 us
  local copies, waits for them, and re-layouts: 159 us -> 0 us
  waiting for transfers between devices: 141 us -> 0.06 us
  other arithmetic: 13.3 us -> 0 us
    dot_general x7 -> x0, matrix products: 387 us -> none  [the longest x4 225 us: by_group(): jnp.einsum('gta,gtb->gab', a, b, preferred_element_type=jnp.float32)]
    pallas_call x0 -> x2, Pallas kernels: none -> 320 us  [the longest x1 210 us: fused(): pl.pallas_call(functools.partial(fused_kernel, n), out_shape=[jax.ShapeDt...]
    unnamed x6 -> x0, local copies, waits for them, and re-layouts: 158 us -> none
    dot_general x3 -> x0, waiting for transfers between devices: 77.3 us -> none  [by_group(): jnp.einsum('gta,gtb->gab', a, b, preferred_element_type=jnp.float32)]
    unnamed x5 -> x1, waiting for transfers between devices: 63.9 us -> 0.05 us
    dot_general x1 -> x0, other arithmetic: 13.3 us -> none  [by_group(): jnp.einsum('gta,gtb->gab', a, b, preferred_element_type=jnp.float32)]
  transfers between devices with their start and end apart: 6 -> 1, of which waited for: 2 -> 0; matrix products, arithmetic and copies ran while one was open for 77% -> 0% of each run, Pallas kernels for 0% -> 33%
where the time goes in v1:
time: 334 us
  Pallas kernels  320 us (96%)
  between operations  14.1 us (4%)
    pallas_call x1, Pallas kernels, fused(): pl.pallas_call(functools.partial(fused_kernel, n), out_shape=[jax.ShapeDt...  210 us
    pallas_call x1, Pallas kernels, weights(): pl.pallas_call(weights_kernel, grid=(nb,), in_specs=[pl.BlockSpec((rows,...  110 us
  transfers between devices with their start and end apart: 1, of which 0 were waited for; matrix products, arithmetic and copies ran while one was open for 0% of the time, Pallas kernels for 33%

profile of v1, /device:TPU:112, one launch (start us, length us, event | category | flops | bytes accessed | tf_op | source)
XLA Modules:
  0.0 334.3 jit_solution(16705391515853117584)
XLA Ops:
  7.2 0.1 reduce-scatter.2.cloned.1.call-start
  7.2 210.1 %fused.1 = (bf16[4480,6656]{1,0:T(8,128)(2,1)}, bf16[18,640,512]{2,1,0:T(8,128)(2,1)}, bf16[640,6656]{1,0:T(8,128)(2,1)}, bf16[640,6656]{1,0:T(8,128)(2,1)}) custom-call(bf16[160,6656]{1,0:T(8,128)(2,1)} %x_own.1, bf16[160,6656]{1,0:T(8,128)(2,1)} %dy_own.1, bf16[640,4480]{1,0:T(8,128)(2,1)} %gate.1, bf16[640,4480]{1,0:T(8,128)(2,1)} %up.1, ...), custom_call_target="tpu_custom_call" | custom-call | flops 152672665600 | bytes 298188800 | tf_op jit(solution)/shard_map/fused/pallas_call | solution.py:403
  217.3 0.1 reduce-scatter.2.cloned.1.call-update
  217.4 110.0 %weights.1 = (bf16[6656,4480]{1,0:T(8,128)(2,1)}, bf16[6656,4480]{1,0:T(8,128)(2,1)}, bf16[4480,6656]{1,0:T(8,128)(2,1)}) custom-call(bf16[640,6656]{1,0:T(8,128)(2,1)} %get-tuple-element.12.x_ref, bf16[18,640,512]{2,1,0:T(8,128)(2,1)} %get-tuple-element.13.dcat_ref, bf16[4480,6656]{1,0:T(8,128)(2,1)} %get-tuple-element.14.dwd_ref), custom_call_target="tpu_custom_call" | custom-call | flops 76336332800 | bytes 238551040 | tf_op jit(solution)/shard_map/weights/pallas_call | solution.py:449
  327.4 0.0 reduce-scatter.2.cloned.1.call-done
Async XLA Ops:
  7.2 320.2 %reduce-scatter.2.cloned.1.call-start = ((), (), s32[]{:S(2)}) async-start(), calls=%async_computation.1 | async-start | bytes 10649600 | tf_op jit(solution)/shard_map/reduce_scatter | solution.py:478
Sparse Core Ops, SparseCore 0:
  217.5 78.9 reduce-scatter.1
